TPU v7x, 32 devices: a whole 2x2x4 slice. The times are simulated.
32 devices in a mesh: fsdp: 4 (over z), ctx: 4 (over y, x), tp: 2 (over core).
Axes of the slice: x: 2, y: 2, z: 4, core: 2. Of those that a mesh axis runs over, the one named last changes fastest.
Arguments:
- block_input: bfloat16 [4, 1024, 1600], P('fsdp', 'ctx'), may hold values from -8 to 8
- segments: int32 [4, 1024], P('fsdp', 'ctx'), may hold values from 0 to 3, never falling along the last dimension, each value on 1 to 512 neighbouring positions
- ln1_gain: float32 [1600], replicated, may hold values from 0.5 to 1.5
- ln1_shift: float32 [1600], replicated, may hold values from -3 to 3
- qkv_weight: bfloat16 [1600, 4800], P('fsdp'), may hold values from -4 to 4
- out_weight: bfloat16 [1600, 1600], P(None, 'fsdp'), may hold values from -0.4375 to 0.4375
- ln2_gain: float32 [1600], replicated, may hold values from 0.5 to 1.5
- ln2_shift: float32 [1600], replicated, may hold values from -3 to 3
- fc_weight: bfloat16 [1600, 6400], P('fsdp', 'tp'), may hold values from -0.15625 to 0.15625
- proj_weight: bfloat16 [6400, 1600], P('tp', 'fsdp'), may hold values from -0.078125 to 0.078125
- cotangent: bfloat16 [4, 1024, 1600], P('fsdp', 'ctx'), may hold values from -6 to 6
Outputs:
- block_output: bfloat16 [4, 1024, 1600], P('fsdp', 'ctx')
- grad_input: float32 [4, 1024, 1600], P('fsdp', 'ctx')
- grad_ln1_gain: float32 [1600], P(('fsdp', 'ctx'))
- grad_ln1_shift: float32 [1600], P(('fsdp', 'ctx'))
- grad_qkv_weight: float32 [1600, 4800], P(('fsdp', 'ctx'))
- grad_out_weight: float32 [1600, 1600], P(None, ('fsdp', 'ctx'))
- grad_ln2_gain: float32 [1600], P(('fsdp', 'ctx'))
- grad_ln2_shift: float32 [1600], P(('fsdp', 'ctx'))
- grad_fc_weight: float32 [1600, 6400], P(('fsdp', 'ctx'), 'tp')
- grad_proj_weight: float32 [6400, 1600], P('tp', ('fsdp', 'ctx'))
All inputs are finite; a program needn't handle non-finite values.
Results may differ from a plain program's by a relative error of at most 0.013.
The roundings to bfloat16 on the way count: a program that leaves them out, or rounds other values in their place, can miss the bound.
Values may be sent and summed in bfloat16 or wider, within the bound.
A program may use at most 320 MiB of HBM per device.

v0:
```python
import jax
import jax.numpy as jnp
from jax import lax
from jax.sharding import PartitionSpec as P

D = 1600
H = 25
HD = 64
norm_epsilon = 1e-05


def normalize(values, norm_gain, norm_shift):
    row_mean = jnp.mean(values, axis=-1, keepdims=True)
    centered = values - row_mean
    inv_std = lax.rsqrt(jnp.mean(centered * centered, axis=-1, keepdims=True) + norm_epsilon)
    normed = centered * inv_std
    return (normed * norm_gain + norm_shift, normed, inv_std)


def norm_back(upstream, normed, inv_std, norm_gain):
    scaled = upstream * norm_gain
    back_grad = inv_std * (
        scaled
        - jnp.mean(scaled, axis=-1, keepdims=True)
        - normed * jnp.mean(scaled * normed, axis=-1, keepdims=True)
    )
    return (back_grad, jnp.sum(upstream * normed, axis=(0, 1)), jnp.sum(upstream, axis=(0, 1)))


def masked_scores(queries, key_rows, query_seg, key_seg, query_pos):
    raw_scores = jnp.einsum("qhd,khd->hqk", queries, key_rows, preferred_element_type=jnp.float32)
    scores = raw_scores * queries.shape[-1] ** (-0.5)
    key_pos = jnp.arange(key_rows.shape[0], dtype=jnp.int32)
    allowed = (key_pos[None, :] <= query_pos[:, None]) & (key_seg[None, :] == query_seg[:, None])
    return jnp.where(allowed[None], scores, -1e30)


def attend(queries, key_rows, value_rows, query_seg, key_seg, query_pos):
    scores = masked_scores(queries, key_rows, query_seg, key_seg, query_pos)
    row_max = jnp.max(scores, axis=-1, keepdims=True)
    exponent = jnp.exp(scores - row_max)
    row_total = jnp.sum(exponent, axis=-1, keepdims=True)
    probabilities = (exponent / row_total).astype(jnp.bfloat16)
    attended = jnp.einsum(
        "hqk,khd->qhd", probabilities, value_rows, preferred_element_type=jnp.float32
    )
    return (attended, row_max + jnp.log(row_total))


def attend_back(
    queries, key_rows, value_rows, query_seg, key_seg, query_pos, log_total, grad_attended
):
    scores = masked_scores(queries, key_rows, query_seg, key_seg, query_pos)
    probabilities = jnp.exp(scores - log_total)
    grad_values = jnp.einsum(
        "hqk,qhd->khd",
        probabilities.astype(jnp.bfloat16),
        grad_attended,
        preferred_element_type=jnp.float32,
    )
    grad_probs = jnp.einsum(
        "qhd,khd->hqk", grad_attended, value_rows, preferred_element_type=jnp.float32
    )
    row_inner = jnp.sum(probabilities * grad_probs, axis=-1, keepdims=True)
    grad_raw = (probabilities * (grad_probs - row_inner) * queries.shape[-1] ** (-0.5)).astype(
        jnp.bfloat16
    )
    grad_query = jnp.einsum("hqk,khd->qhd", grad_raw, key_rows, preferred_element_type=jnp.float32)
    grad_keys = jnp.einsum("hqk,qhd->khd", grad_raw, queries, preferred_element_type=jnp.float32)
    return (grad_query, grad_keys, grad_values)


def slots_of(member, head_slots, tp_size):
    first_head = member * H // tp_size
    last_head = (member + 1) * H // tp_size
    wanted = first_head + jnp.arange(head_slots, dtype=jnp.int32)
    slot_heads = jnp.minimum(wanted, H - 1)
    slot_valid = (wanted < last_head).astype(jnp.float32)
    return (slot_heads, slot_valid)


def gelu_tanh(values):
    return jax.nn.gelu(values, approximate=True)


def local(
    block_input,
    segments,
    ln1_gain,
    ln1_shift,
    qkv_weight,
    out_weight,
    ln2_gain,
    ln2_shift,
    fc_weight,
    proj_weight,
    cotangent,
):
    tp_size = lax.axis_size("tp")
    tp_rank = lax.axis_index("tp")
    head_slots = (H + tp_size - 1) // tp_size
    slot_heads, slot_valid = slots_of(tp_rank, head_slots, tp_size)
    gathered = (
        lax.all_gather(qkv_weight, "fsdp", axis=0, tiled=True),
        lax.all_gather(out_weight, "fsdp", axis=1, tiled=True),
        lax.all_gather(fc_weight, "fsdp", axis=0, tiled=True),
        lax.all_gather(proj_weight, "fsdp", axis=1, tiled=True),
    )
    matrix = gathered[0]
    row_count = matrix.shape[0]
    query_key_value_weight = jnp.take(
        matrix.reshape(row_count, 3, H, HD), slot_heads, axis=2
    ).reshape(row_count, 3 * head_slots * HD)
    matrix = gathered[1]
    col_count = matrix.shape[1]
    contract_weight = jnp.take(matrix.reshape(H, HD, col_count), slot_heads, axis=0).reshape(
        head_slots * HD, col_count
    )
    expand_weight = gathered[2]
    attention_projection_weight = gathered[3]
    head_select_mask = jnp.repeat(slot_valid, HD).astype(jnp.bfloat16)
    contract_weight = contract_weight * head_select_mask[:, None]
    seq_count, local_len, model_width = block_input.shape
    input_f32 = block_input.astype(jnp.float32)
    hidden_one, normed_one, inv_one = normalize(input_f32, ln1_gain, ln1_shift)
    first_hidden_reduced = hidden_one.astype(jnp.bfloat16)
    qkv_values = jnp.einsum(
        "iwq,qr->iwr",
        first_hidden_reduced,
        query_key_value_weight,
        preferred_element_type=jnp.float32,
    ).astype(jnp.bfloat16)
    qkv_values = qkv_values.reshape(seq_count, local_len, 3, head_slots, HD)
    queries = qkv_values[:, :, 0]
    kv_local = jnp.stack([qkv_values[:, :, 1], qkv_values[:, :, 2]])
    seg_low = segments.astype(jnp.bfloat16)
    kv_all, seg_all = (
        lax.all_gather(kv_local, "ctx", axis=2, tiled=True),
        lax.all_gather(seg_low, "ctx", axis=1, tiled=True),
    )
    query_pos = lax.axis_index("ctx") * local_len + jnp.arange(local_len, dtype=jnp.int32)
    attended, log_total = lax.map(
        lambda entry: attend(entry[0], entry[1], entry[2], entry[3], entry[4], query_pos),
        (queries, kv_all[0], kv_all[1], seg_low, seg_all),
    )
    attention_output_reduced = attended.astype(jnp.bfloat16).reshape(
        seq_count, local_len, head_slots * HD
    )
    attn_sum = lax.psum(
        jnp.einsum(
            "qwa,ap->qwp",
            attention_output_reduced,
            contract_weight,
            preferred_element_type=jnp.float32,
        ),
        "tp",
    )
    residual_one = input_f32 + attn_sum
    hidden_two, normed_two, inv_two = normalize(residual_one, ln2_gain, ln2_shift)
    second_hidden_reduced = hidden_two.astype(jnp.bfloat16)
    pre_act = jnp.einsum(
        "whv,vi->whi", second_hidden_reduced, expand_weight, preferred_element_type=jnp.float32
    )
    activation, gelu_pull = jax.vjp(gelu_tanh, pre_act)
    activation_reduced = activation.astype(jnp.bfloat16)
    mlp_sum = lax.psum(
        jnp.einsum(
            "ojk,kg->ojg",
            activation_reduced,
            attention_projection_weight,
            preferred_element_type=jnp.float32,
        ).astype(jnp.bfloat16),
        "tp",
    ).astype(jnp.float32)
    result = (residual_one + mlp_sum).astype(jnp.bfloat16)
    grad_output = cotangent.astype(jnp.float32)
    projection_gradient = jnp.einsum(
        "xbi,xbm->im", activation_reduced, cotangent, preferred_element_type=jnp.float32
    )
    activation_gradient = jnp.einsum(
        "tua,ya->tuy", cotangent, attention_projection_weight, preferred_element_type=jnp.float32
    )
    preactivation_gradient = gelu_pull(activation_gradient)[0].astype(jnp.bfloat16)
    grad_fc = jnp.einsum(
        "atm,atk->mk",
        second_hidden_reduced,
        preactivation_gradient,
        preferred_element_type=jnp.float32,
    )
    grad_h2 = lax.psum(
        jnp.einsum(
            "kau,gu->kag", preactivation_gradient, expand_weight, preferred_element_type=jnp.float32
        ),
        "tp",
    )
    back_two, grad_g2, grad_s2 = norm_back(grad_h2, normed_two, inv_two, ln2_gain)
    grad_r1 = grad_output + back_two
    attention_gradient = grad_r1.astype(jnp.bfloat16)
    grad_out_local = jnp.einsum(
        "izy,izr->yr",
        attention_output_reduced * head_select_mask,
        attention_gradient,
        preferred_element_type=jnp.float32,
    )
    grad_attended = jnp.einsum(
        "gmi,ti->gmt", attention_gradient, contract_weight, preferred_element_type=jnp.float32
    )
    grad_attended = grad_attended.astype(jnp.bfloat16).reshape(seq_count, local_len, head_slots, HD)
    grad_query, grad_keys, grad_values = lax.map(
        lambda entry: attend_back(
            entry[0], entry[1], entry[2], entry[3], entry[4], query_pos, entry[5], entry[6]
        ),
        (queries, kv_all[0], kv_all[1], seg_low, seg_all, log_total, grad_attended),
    )
    kv_grad = lax.psum_scatter(
        jnp.stack([grad_keys, grad_values]).astype(jnp.bfloat16),
        "ctx",
        scatter_dimension=2,
        tiled=True,
    ).astype(jnp.float32)
    query_key_value_gradient = jnp.stack([grad_query, kv_grad[0], kv_grad[1]], axis=2).astype(
        jnp.bfloat16
    )
    query_key_value_gradient = query_key_value_gradient.reshape(
        seq_count, local_len, 3 * head_slots * HD
    )
    grad_qkv_local = jnp.einsum(
        "axy,axh->yh",
        first_hidden_reduced,
        query_key_value_gradient,
        preferred_element_type=jnp.float32,
    )
    grad_h1 = lax.psum(
        jnp.einsum(
            "cbz,iz->cbi",
            query_key_value_gradient,
            query_key_value_weight,
            preferred_element_type=jnp.float32,
        ),
        "tp",
    )
    back_one, grad_g1, grad_s1 = norm_back(grad_h1, normed_one, inv_one, ln1_gain)
    grad_total = grad_r1 + back_one
    qkv_full = (
        jnp.zeros((D, 3, H, HD), jnp.float32)
        .at[:, :, slot_heads, :]
        .add(grad_qkv_local.reshape(D, 3, head_slots, HD))
    )
    out_full = (
        jnp.zeros((H, HD, D), jnp.float32)
        .at[slot_heads]
        .add(grad_out_local.reshape(head_slots, HD, D))
    )
    partial_value = (
        lax.psum_scatter(
            qkv_full.reshape(D, 3 * H * HD), ("fsdp", "ctx"), scatter_dimension=0, tiled=True
        ),
        lax.psum_scatter(
            out_full.reshape(H * HD, D), ("fsdp", "ctx"), scatter_dimension=1, tiled=True
        ),
    )
    qkv_grad_out, out_grad_out = (
        lax.psum(partial_value[0].astype(jnp.bfloat16), "tp").astype(jnp.float32),
        lax.psum(partial_value[1].astype(jnp.bfloat16), "tp").astype(jnp.float32),
    )
    unit_sums = (
        lax.psum_scatter(grad_fc, ("fsdp", "ctx"), scatter_dimension=0, tiled=True),
        lax.psum_scatter(projection_gradient, ("fsdp", "ctx"), scatter_dimension=1, tiled=True),
        lax.psum_scatter(grad_g1, ("fsdp", "ctx"), scatter_dimension=0, tiled=True),
        lax.psum_scatter(grad_s1, ("fsdp", "ctx"), scatter_dimension=0, tiled=True),
        lax.psum_scatter(grad_g2, ("fsdp", "ctx"), scatter_dimension=0, tiled=True),
        lax.psum_scatter(grad_s2, ("fsdp", "ctx"), scatter_dimension=0, tiled=True),
    )
    return (
        result,
        grad_total,
        unit_sums[2],
        unit_sums[3],
        qkv_grad_out,
        out_grad_out,
        unit_sums[4],
        unit_sums[5],
        unit_sums[0],
        unit_sums[1],
    )


def solution(mesh):
    placed = (
        P("fsdp", "ctx", None),
        P("fsdp", "ctx"),
        P(),
        P(),
        P("fsdp", None),
        P(None, "fsdp"),
        P(),
        P(),
        P("fsdp", "tp"),
        P("tp", "fsdp"),
        P("fsdp", "ctx", None),
    )
    return jax.shard_map(
        local,
        mesh=mesh,
        in_specs=placed,
        out_specs=(
            P("fsdp", "ctx", None),
            P("fsdp", "ctx", None),
            P(("fsdp", "ctx")),
            P(("fsdp", "ctx")),
            P(("fsdp", "ctx"), None),
            P(None, ("fsdp", "ctx")),
            P(("fsdp", "ctx")),
            P(("fsdp", "ctx")),
            P(("fsdp", "ctx"), "tp"),
            P("tp", ("fsdp", "ctx")),
        ),
        check_vma=False,
    )
```

profile of v0, /device:TPU:0, one launch (start us, length us, event | category | flops | bytes accessed | tf_op | source)
XLA Modules:
  0.0 3262.2 jit_solution(14725272297948683888)
XLA Ops:
  9.3 269.9 %all-gather.6.cloned.1.call-done = bf16[1600,4800]{1,0:T(8,128)(2,1)} async-done(((bf16[400,4800]{1,0:T(8,128)(2,1)}), bf16[1600,4800]{1,0:T(8,128)(2,1)}) %all-gather.6.cloned.1.call-update) | async-done | bytes 15360016 | tf_op jit(solution)/shard_map/all_gather | solution.py:104
  279.3 22.4 copy.30
  301.6 13.5 copy.31
  315.1 10.7 gather_fusion
  348.0 8.2 all_gather.22
  356.6 21.8 all-gather.10.cloned.1.call-done
  378.4 9.6 copy.33
  396.9 28.2 all-gather.8.cloned.1.call-done
  453.8 16.0 all-reduce.20.cloned.1.call-done
  471.8 180.5 %all-gather.12.cloned.1.call-done = bf16[1600,3200]{1,0:T(8,128)(2,1)} async-done(((bf16[400,3200]{1,0:T(8,128)(2,1)}), bf16[1600,3200]{1,0:T(8,128)(2,1)}) %all-gather.12.cloned.1.call-update) | async-done | bytes 10240016 | tf_op jit(solution)/shard_map/all_gather | solution.py:106
  652.3 9.1 fusion.86
  661.4 170.5 %all-gather.14.cloned.1.call-done = bf16[3200,1600]{0,1:T(8,128)(2,1)} async-done(((bf16[3200,400]{0,1:T(8,128)(2,1)}), bf16[3200,1600]{0,1:T(8,128)(2,1)}) %all-gather.14.cloned.1.call-update) | async-done | bytes 10240016 | tf_op jit(solution)/shard_map/all_gather | solution.py:107
  831.8 9.8 fusion.26
  847.3 10.8 fusion.66
  858.1 9.2 fusion.84
  873.7 8.5 fusion.48
  889.0 26.9 fusion.51
  920.1 961.2 %fusion.88 = (f32[112,3200]{1,0:T(8,128)}, f32[3200,112]{0,1:T(8,128)S(1)}) fusion(f32[1600,3200]{1,0:T(8,128)} %fusion.84, f32[3200,1600]{0,1:T(8,128)} %fusion.66), kind=kCustom, calls=%all-reduce-scatter.3 | all-reduce-scatter fusion | flops 11468801 | bytes 43827712
  1894.3 25.5 fusion.55
  1921.2 8.4 convolution_bitcast_fusion
  1929.6 7.9 convolution_bitcast_fusion.1
  1937.6 11.4 copy.34
  1949.0 10.9 broadcast_in_dim.115
  1960.0 33.4 %scatter_fusion = f32[1600,3,25,64]{0,3,2,1:T(8,128)} fusion(f32[1600,3,25,64]{0,3,2,1:T(8,128)} %broadcast_in_dim.115, s32[13]{0:T(128)S(1)} %copy-done.27, f32[13,1600,3,64]{1,3,2,0:T(8,128)} %copy.34), kind=kCustom, calls=%fused_computation.2 | custom fusion | flops 3993600 | bytes 47923252 | tf_op jit(solution)/shard_map/scatter-add | solution.py:247
  1993.4 34.2 %copy.35 = f32[1600,4800]{1,0:T(8,128)} copy(f32[1600,4800]{0,1:T(8,128)} %bitcast.129) | data formatting | bytes 61440000 | tf_op jit(solution)/shard_map/reshape | solution.py:256
  2027.6 671.4 %fusion = f32[104,4800]{1,0:T(8,128)} fusion(f32[1600,4800]{1,0:T(8,128)} %copy.35), kind=kCustom, calls=%all-reduce-scatter | all-reduce-scatter fusion | flops 7987201 | bytes 32717312
  2702.9 8.9 fusion.27
  2720.3 15.3 scatter_fusion.1
  2735.6 9.3 concatenate.17
  2749.8 459.8 %all-reduce.27 = (bf16[1600,1600]{1,0:T(8,128)(2,1)}, f32[1600]{0:T(1024)S(1)}, f32[1600]{0:T(1024)S(1)}, f32[1600]{0:T(1024)S(1)}, f32[1600]{0:T(1024)S(1)}) all-reduce(f32[1600,1600]{1,0:T(8,128)} %bitcast.130, f32[1600]{0:T(1024)S(1)} %get-tuple-element.95, ...), channel_id=6, replica_groups=mesh['fsdp'=4,'ctx'=4,'tp'=2] {'fsdp','ctx'}, use_global_device_ids=true, to_apply=%region_24.25.clone | all-reduce | flops 2566400 | bytes 15411200
  3212.3 14.7 concatenate.18
  3227.0 13.9 concatenate.19
  (156 shorter events, 133.5 us)
Async XLA Ops:
  7.2 272.1 %all-gather.6.cloned.1.call-start = ((), (), s32[]{:S(2)}) async-start(), calls=%async_computation.1 | async-start | bytes 19456000 | tf_op jit(solution)/shard_map/all_gather | solution.py:104
  7.9 370.5 %all-gather.10.cloned.1.call-start = ((), (), s32[]{:S(2)}) async-start(), calls=%async_computation.3 | async-start | bytes 6656000 | tf_op jit(solution)/shard_map/all_gather | solution.py:105
  8.7 416.4 %all-gather.8.cloned.1.call-start = ((), (), s32[]{:S(2)}) async-start(), calls=%async_computation.2 | async-start | bytes 4259840 | tf_op jit(solution)/shard_map/all_gather | solution.py:138
  8.7 292.9 %copy-start.26 = (s32[13]{0:T(128)}, s32[13]{0:T(128)S(1)}, u32[]{:S(2)}) copy-start(s32[13]{0:T(128)S(1)} %fusion.77) | copy-start | bytes 160
  333.3 7.3 copy-start.22
  333.3 7.3 copy-start.25
  346.6 78.5 %copy-start.17 = (bf16[256,2496]{0,1:T(8,128)(2,1)}, bf16[256,2496]{0,1:T(8,128)(2,1)S(1)}, u32[]{:S(2)}) copy-start(bf16[256,2496]{0,1:T(8,128)(2,1)S(1)} %convolution_convert_fusion) | copy-start | bytes 3833860
  347.9 121.9 %all-reduce.20.cloned.1.call-start = ((), (), s32[]{:S(2)}) async-start(), calls=%async_computation.4 | async-start | bytes 3276800 | tf_op jit(solution)/shard_map/psum | solution.py:149
  432.7 7.3 copy-start.12
  449.1 203.1 %all-gather.12.cloned.1.call-start = ((), (), s32[]{:S(2)}) async-start(), calls=%async_computation.5 | async-start | bytes 12800000 | tf_op jit(solution)/shard_map/all_gather | solution.py:106
  449.7 382.1 %all-gather.14.cloned.1.call-start = ((), (), s32[]{:S(2)}) async-start(), calls=%async_computation.6 | async-start | bytes 12800000 | tf_op jit(solution)/shard_map/all_gather | solution.py:107
  450.3 417.0 %all-reduce.22.cloned.1.call-start = ((), (), s32[]{:S(2)}) async-start(), calls=%async_computation.7 | async-start | bytes 3276800 | tf_op jit(solution)/shard_map/psum | solution.py:190
  452.8 199.4 %copy-start.19 = (f32[1600]{0:T(1024)S(1)}, f32[1600]{0:T(1024)}, u32[]{:S(2)}) copy-start(f32[1600]{0:T(1024)} %param.17) | copy-start | bytes 19204
  452.8 199.4 %copy-start.21 = (f32[1600]{0:T(1024)S(1)}, f32[1600]{0:T(1024)}, u32[]{:S(2)}) copy-start(f32[1600]{0:T(1024)} %param.18) | copy-start | bytes 19204
  471.5 398.9 %copy-start = (f32[1,256,1600]{1,2,0:T(8,128)}, f32[1,256,1600]{1,2,0:T(8,128)S(1)}, u32[]{:S(2)}) copy-start(f32[1,256,1600]{1,2,0:T(8,128)S(1)} %get-tuple-element.114) | copy-start | bytes 4915204
  471.7 360.1 %copy-start.11 = (bf16[1,256,1600]{1,2,0:T(8,128)(2,1)S(1)}, bf16[1,256,1600]{1,2,0:T(8,128)(2,1)}, u32[]{:S(2)}) copy-start(bf16[1,256,1600]{1,2,0:T(8,128)(2,1)} %param.21) | copy-start | bytes 2457604
  831.8 11.0 copy-start.3
  847.0 1072.8 %reduce-scatter.9.cloned.1.call-start = ((), (), s32[]{:S(2)}) async-start(), calls=%async_computation.8 | async-start | bytes 4259840 | tf_op jit(solution)/shard_map/reduce_scatter | solution.py:215
  847.3 10.9 copy-start.16
  873.7 8.5 copy-start.13
  920.1 1827.3 %all-reduce.24.cloned.1.call-start = ((), (), s32[]{:S(2)}) async-start(), calls=%async_computation.9 | async-start | bytes 3276800 | tf_op jit(solution)/shard_map/psum | solution.py:233
  1883.5 1328.8 %collective-permute-start.1 = (f32[112,3200]{1,0:T(8,128)}, f32[112,3200]{1,0:T(8,128)}, u32[]{:S(2)}, u32[]{:S(2)}) collective-permute-start(f32[112,3200]{1,0:T(8,128)} %get-tuple-element.111), channel_id=1, source_target_pairs={{0,2},{2,4},{4,6},{6,8},{8,10},{10,12},{12,14},{14,16},{16,18},{18... | collective-permute-start | bytes 4300808
  1887.0 1340.0 %collective-permute-start.3 = (f32[3200,112]{0,1:T(8,128)S(1)}, f32[3200,112]{0,1:T(8,128)}, u32[]{:S(2)}, u32[]{:S(2)}) collective-permute-start(f32[3200,112]{0,1:T(8,128)S(1)} %get-tuple-element.112), channel_id=1, source_target_pairs={{0,2},{2,4},{4,6},{6,8},{8,10},{10,12},{12,14},{14,16},{16,18},{18... | collective-permute-start | bytes 4300808
  1889.4 1337.6 %collective-permute-start.4 = (f32[3200,68]{0,1:T(8,128)}, f32[3200,68]{0,1:T(8,128)}, u32[]{:S(2)}, u32[]{:S(2)}) collective-permute-start(f32[3200,68]{0,1:T(8,128)} %slice.43), channel_id=1, source_target_pairs={{0,4},{2,6},{4,8},{6,10},{8,12},{10,14},{12,16},{14,18},{16,20},{1... | collective-permute-start | bytes 2611208
  1892.1 1320.2 %collective-permute-start.2 = (f32[68,3200]{1,0:T(8,128)}, f32[68,3200]{1,0:T(8,128)}, u32[]{:S(2)}, u32[]{:S(2)}) collective-permute-start(f32[68,3200]{1,0:T(8,128)} %slice.42), channel_id=1, source_target_pairs={{0,4},{2,6},{4,8},{6,10},{8,12},{10,14},{12,16},{14,18},{16,20},{1... | collective-permute-start | bytes 2611208
  1937.6 1312.5 %all-reduce.26.cloned.1.call-start = ((), (), s32[]{:S(2)}) async-start(), calls=%async_computation.10 | async-start | bytes 4481024 | tf_op jit(solution)/shard_map/psum | solution.py:264
  1949.0 11.0 copy-start.27
  2701.2 10.6 copy-start.5
  2701.2 10.6 copy-start.14
  2701.2 34.4 %collective-permute-start = (bf16[60,4800]{1,0:T(8,128)(2,1)}, bf16[60,4800]{1,0:T(8,128)(2,1)S(1)}, u32[]{:S(2)}, u32[]{:S(2)}) collective-permute-start(bf16[60,4800]{1,0:T(8,128)(2,1)} %slice.41), channel_id=1, source_target_pairs={{0,2},{2,4},{4,6},{6,8},{8,10},{10,12},{12,14},{14,16},{16,18},{18... | collective-permute-start | bytes 1728008
  3240.9 7.6 copy-start.6
  3240.9 7.6 copy-start.9
  (13 other events, 40.1 us)
Sparse Core Ops, SparseCore 0:
  9.6 269.6 all-gather.5
  280.8 97.5 all-gather.9
  380.8 44.2 all-gather.7
  449.3 20.4 all-reduce.19
  471.2 181.0 all-gather.11
  653.7 178.0 all-gather.13
  847.2 18.6 all-reduce.21
  920.2 149.3 reduce-scatter.8
  1937.7 32.3 all-reduce.23
  3211.8 20.5 all-reduce.25
where the time goes:
time: 3270 us; the launch traced here: 3260 us
  blocking collectives  2100 us (64%)
  waiting for transfers between devices  689 us (21%)
  local copies, waits for them, and re-layouts  192 us (6%)
  matrix products  163 us (5%)
  other arithmetic  87.7 us (3%)
    unnamed x3, blocking collectives  2090 us
    all_gather x1, waiting for transfers between devices, local(): lax.all_gather(qkv_weight, 'fsdp', axis=0, tiled=True)  270 us
    all_gather x1, waiting for transfers between devices, local(): lax.all_gather(fc_weight, 'fsdp', axis=0, tiled=True)  181 us
    all_gather x1, waiting for transfers between devices, local(): lax.all_gather(proj_weight, 'fsdp', axis=1, tiled=True)  170 us
  transfers between devices with their start and end apart: 15, of which 6 were waited for; matrix products, arithmetic and copies ran while one was open for 61% of the time, Pallas kernels for 0%

commit v1 on v0

--- a/solution.py
+++ b/solution.py
@@ -7,6 +7,24 @@
 H = 25
 HD = 64
 norm_epsilon = 1e-05
+
+
+def ring_gather(shard, axis, dim):
+    ways, here, turn = (lax.axis_size(axis), lax.axis_index(axis), shard.shape[dim])
+    shape = [n * ways if d == dim else n for d, n in enumerate(shard.shape)]
+    full = lax.dynamic_update_slice_in_dim(
+        jnp.zeros(shape, shard.dtype), shard, here * turn, axis=dim
+    )
+    going_up = going_down = shard
+    for far in range(1, ways // 2 + 1):
+        going_up = lax.ppermute(going_up, axis, [(d, (d + 1) % ways) for d in range(ways)])
+        full = lax.dynamic_update_slice_in_dim(full, going_up, (here - far) % ways * turn, axis=dim)
+        if 2 * far < ways:
+            going_down = lax.ppermute(going_down, axis, [(d, (d - 1) % ways) for d in range(ways)])
+            full = lax.dynamic_update_slice_in_dim(
+                full, going_down, (here + far) % ways * turn, axis=dim
+            )
+    return full
 
 
 def normalize(values, norm_gain, norm_shift):
@@ -104,7 +122,7 @@
         lax.all_gather(qkv_weight, "fsdp", axis=0, tiled=True),
         lax.all_gather(out_weight, "fsdp", axis=1, tiled=True),
         lax.all_gather(fc_weight, "fsdp", axis=0, tiled=True),
-        lax.all_gather(proj_weight, "fsdp", axis=1, tiled=True),
+        ring_gather(proj_weight, "fsdp", 1),
     )
     matrix = gathered[0]
     row_count = matrix.shape[0]

time: 3270 us -> 3310 us (1.012)
  waiting for transfers between devices: 689 us -> 617 us
  starting transfers between devices: 12.5 us -> 81.6 us
    ppermute x0 -> x3, waiting for transfers between devices: none -> 229 us  [the longest x2 125 us: ring_gather(): lax.ppermute(going_up, axis, [(d, (d + 1) % ways) for d in range(ways)])]
    all_gather x1 -> x0, waiting for transfers between devices: 170 us -> none  [local(): lax.all_gather(proj_weight, 'fsdp', axis=1, tiled=True)]
    all_gather x1, waiting for transfers between devices: 181 us -> 25.4 us  [local(): lax.all_gather(fc_weight, 'fsdp', axis=0, tiled=True)]
    ppermute x0 -> x3, starting transfers between devices: none -> 58.2 us  [the longest x2 55.9 us: ring_gather(): lax.ppermute(going_up, axis, [(d, (d + 1) % ways) for d in range(ways)])]
    psum x1, waiting for transfers between devices: 0.01 us -> 39.7 us  [local(): lax.psum(partial_value[1].astype(jnp.bfloat16), 'tp').astype(jnp.float32)]
  transfers between devices with their start and end apart: 15 -> 17, of which waited for: 6 -> 9; matrix products, arithmetic and copies ran while one was open for 61% -> 60% of each run, Pallas kernels for 0% -> 0%
where the time goes in v1:
time: 3310 us; the launch traced here: 3290 us
  blocking collectives  2120 us (64%)
  waiting for transfers between devices  617 us (19%)
  local copies, waits for them, and re-layouts  209 us (6%)
  matrix products  163 us (5%)
  other arithmetic  87.7 us (3%)
  starting transfers between devices  81.6 us (2%)
    unnamed x3, blocking collectives  2110 us
    all_gather x1, waiting for transfers between devices, local(): lax.all_gather(qkv_weight, 'fsdp', axis=0, tiled=True)  270 us
    ppermute x2, waiting for transfers between devices, ring_gather(): lax.ppermute(going_up, axis, [(d, (d + 1) % ways) for d in range(ways)])  125 us
    ppermute x1, waiting for transfers between devices, ring_gather(): lax.ppermute(going_down, axis, [(d, (d - 1) % ways) for d in range(ways)])  104 us
  transfers between devices with their start and end apart: 17, of which 9 were waited for; matrix products, arithmetic and copies ran while one was open for 60% of the time, Pallas kernels for 0%

profile of v1, /device:TPU:0, one launch (start us, length us, event | category | flops | bytes accessed | tf_op | source)
XLA Modules:
  0.0 3289.9 jit_solution(9248484667686018520)
XLA Ops:
  9.3 269.9 %all-gather.5.cloned.1.call-done = bf16[1600,4800]{1,0:T(8,128)(2,1)} async-done(((bf16[400,4800]{1,0:T(8,128)(2,1)}), bf16[1600,4800]{1,0:T(8,128)(2,1)}) %all-gather.5.cloned.1.call-update) | async-done | bytes 15360016 | tf_op jit(solution)/shard_map/all_gather | solution.py:122
  279.3 22.4 copy.32
  301.7 13.5 copy.33
  315.2 10.7 gather_fusion
  356.8 21.6 all-gather.9.cloned.1.call-done
  378.4 9.4 copy.35
  396.9 28.2 all-gather.7.cloned.1.call-done
  453.7 80.1 %collective-permute-done = bf16[3200,400]{0,1:T(8,128)(2,1)} collective-permute-done((bf16[3200,400]{0,1:T(8,128)(2,1)}, bf16[3200,400]{0,1:T(8,128)(2,1)}, u32[]{:S(2)}, u32[]{:S(2)}) %collective-permute-start) | collective-permute-done | bytes 2560032 | tf_op jit(solution)/shard_map/ppermute | solution.py:20
  533.8 54.3 %collective-permute-start.2 = (bf16[3200,400]{0,1:T(8,128)(2,1)}, bf16[3200,400]{0,1:T(8,128)(2,1)}, u32[]{:S(2)}, u32[]{:S(2)}) collective-permute-start(bf16[3200,400]{0,1:T(8,128)(2,1)} %collective-permute-done), channel_id=1, source_target_pairs={{0,8},{8,16},{16,24},{24,0},{1,9},{9,17},{17,25},{25,1},{2,10},{10... | collective-permute-start | bytes 7680008 | tf_op jit(solution)/shard_map/ppermute | solution.py:20
  599.8 104.0 %collective-permute-done.1 = bf16[3200,400]{0,1:T(8,128)(2,1)} collective-permute-done((bf16[3200,400]{0,1:T(8,128)(2,1)}, bf16[3200,400]{0,1:T(8,128)(2,1)}, u32[]{:S(2)}, u32[]{:S(2)}) %collective-permute-start.1) | collective-permute-done | bytes 2560032 | tf_op jit(solution)/shard_map/ppermute | solution.py:23
  707.2 44.8 %collective-permute-done.2 = bf16[3200,400]{0,1:T(8,128)(2,1)} collective-permute-done((bf16[3200,400]{0,1:T(8,128)(2,1)}, bf16[3200,400]{0,1:T(8,128)(2,1)}, u32[]{:S(2)}, u32[]{:S(2)}) %collective-permute-start.2) | collective-permute-done | bytes 2560032 | tf_op jit(solution)/shard_map/ppermute | solution.py:20
  758.3 25.4 all-gather.11.cloned.1.call-done
  791.3 10.4 fusion.26
  807.4 11.1 fusion.66
  818.4 9.2 fusion.81
  835.5 8.5 fusion.48
  850.8 26.8 fusion.51
  881.8 961.2 %fusion.85 = (f32[112,3200]{1,0:T(8,128)}, f32[3200,112]{0,1:T(8,128)S(1)}) fusion(f32[1600,3200]{1,0:T(8,128)} %fusion.81, f32[3200,1600]{0,1:T(8,128)} %fusion.66), kind=kCustom, calls=%all-reduce-scatter.3 | all-reduce-scatter fusion | flops 11468801 | bytes 43827712
  1843.0 25.5 fusion.55
  1886.2 11.4 copy.37
  1897.6 10.8 broadcast_in_dim.119
  1908.4 33.6 %scatter_fusion = f32[1600,3,25,64]{0,3,2,1:T(8,128)} fusion(f32[1600,3,25,64]{0,3,2,1:T(8,128)} %broadcast_in_dim.119, s32[13]{0:T(128)S(1)} %copy-done.28, f32[13,1600,3,64]{1,3,2,0:T(8,128)} %copy.37), kind=kCustom, calls=%fused_computation.2 | custom fusion | flops 3993600 | bytes 47923252 | tf_op jit(solution)/shard_map/scatter-add | solution.py:265
  1942.0 34.2 %copy.38 = f32[1600,4800]{1,0:T(8,128)} copy(f32[1600,4800]{0,1:T(8,128)} %bitcast.131) | data formatting | bytes 61440000 | tf_op jit(solution)/shard_map/reshape | solution.py:274
  1976.1 660.8 %fusion = f32[104,4800]{1,0:T(8,128)} fusion(f32[1600,4800]{1,0:T(8,128)} %copy.38), kind=kCustom, calls=%all-reduce-scatter | all-reduce-scatter fusion | flops 7987201 | bytes 32717312
  2641.6 8.9 fusion.27
  2661.2 13.2 collective-permute-start.5
  2683.0 15.2 scatter_fusion.1
  2698.1 11.6 concatenate.17
  2714.5 485.5 %all-reduce.27 = (bf16[1600,1600]{1,0:T(8,128)(2,1)}, f32[1600]{0:T(1024)S(1)}, f32[1600]{0:T(1024)S(1)}, f32[1600]{0:T(1024)S(1)}, f32[1600]{0:T(1024)S(1)}) all-reduce(f32[1600,1600]{1,0:T(8,128)} %bitcast.132, f32[1600]{0:T(1024)S(1)} %get-tuple-element.95, ...), channel_id=6, replica_groups=mesh['fsdp'=4,'ctx'=4,'tp'=2] {'fsdp','ctx'}, use_global_device_ids=true, to_apply=%region_24.25.clone | all-reduce | flops 2566400 | bytes 15411200
  3202.7 14.5 concatenate.18
  3217.3 12.1 concatenate.19
  3238.7 39.7 %all-reduce.26.cloned.1.call-done = (bf16[1600,100]{1,0:T(8,128)(2,1)}, bf16[1,256,1600]{1,2,0:T(8,128)(2,1)}, bf16[100,4800]{1,0:T(8,128)(2,1)}) async-done(((bf16[1600,100]{1,0:T(8,128)(2,1)}, bf16[1,256,1600]{1,2,0:T(8,128)(2,1)}, bf16[100,4800]{1,0:T(8,128)(2,1)}), (bf16[1600,100]{1,0:T(8,128)(2,1)}, bf16[1,256,1600]{1,2,0:T(8,128)(2,1)}, bf16[100,4800]{1,0:T(8,128)(2,1)})) %all-reduce.26.cloned.1.call-update) | async-done | bytes 2099216 | tf_op jit(solution)/shard_map/psum | solution.py:282
  (173 shorter events, 185.2 us)
Async XLA Ops:
  7.2 272.1 %all-gather.5.cloned.1.call-start = ((), (), s32[]{:S(2)}) async-start(), calls=%async_computation.1 | async-start | bytes 19456000 | tf_op jit(solution)/shard_map/all_gather | solution.py:122
  7.9 370.5 %all-gather.9.cloned.1.call-start = ((), (), s32[]{:S(2)}) async-start(), calls=%async_computation.3 | async-start | bytes 6656000 | tf_op jit(solution)/shard_map/all_gather | solution.py:123
  8.7 416.4 %all-gather.7.cloned.1.call-start = ((), (), s32[]{:S(2)}) async-start(), calls=%async_computation.2 | async-start | bytes 4259840 | tf_op jit(solution)/shard_map/all_gather | solution.py:156
  8.7 292.9 %copy-start.27 = (s32[13]{0:T(128)}, s32[13]{0:T(128)S(1)}, u32[]{:S(2)}) copy-start(s32[13]{0:T(128)S(1)} %fusion.74) | copy-start | bytes 160
  346.9 78.2 %copy-start.18 = (bf16[256,2496]{0,1:T(8,128)(2,1)}, bf16[256,2496]{0,1:T(8,128)(2,1)S(1)}, u32[]{:S(2)}) copy-start(bf16[256,2496]{0,1:T(8,128)(2,1)S(1)} %convolution_convert_fusion) | copy-start | bytes 3833860
  348.1 408.3 %all-reduce.20.cloned.1.call-start = ((), (), s32[]{:S(2)}) async-start(), calls=%async_computation.4 | async-start | bytes 3276800 | tf_op jit(solution)/shard_map/psum | solution.py:167
  449.1 139.2 %copy-start.29 = (u32[32]{0:T(128)S(1)}, u32[32]{0:T(128)}, u32[]{:S(2)}) copy-start(u32[32]{0:T(128)} %constant.182) | copy-start | bytes 388
  449.2 334.5 %all-gather.11.cloned.1.call-start = ((), (), s32[]{:S(2)}) async-start(), calls=%async_computation.5 | async-start | bytes 12800000 | tf_op jit(solution)/shard_map/all_gather | solution.py:124
  449.8 379.4 %all-reduce.22.cloned.1.call-start = ((), (), s32[]{:S(2)}) async-start(), calls=%async_computation.6 | async-start | bytes 3276800 | tf_op jit(solution)/shard_map/psum | solution.py:208
  449.8 84.0 %collective-permute-start = (bf16[3200,400]{0,1:T(8,128)(2,1)}, bf16[3200,400]{0,1:T(8,128)(2,1)}, u32[]{:S(2)}, u32[]{:S(2)}) collective-permute-start(bf16[3200,400]{0,1:T(8,128)(2,1)} %param.20), channel_id=1, source_target_pairs={{0,8},{8,16},{16,24},{24,0},{1,9},{9,17},{17,25},{25,1},{2,10},{10... | collective-permute-start | bytes 7680008 | tf_op jit(solution)/shard_map/ppermute | solution.py:20
  451.3 252.4 %collective-permute-start.1 = (bf16[3200,400]{0,1:T(8,128)(2,1)}, bf16[3200,400]{0,1:T(8,128)(2,1)}, u32[]{:S(2)}, u32[]{:S(2)}) collective-permute-start(bf16[3200,400]{0,1:T(8,128)(2,1)} %param.20), channel_id=1, source_target_pairs={{0,24},{8,0},{16,8},{24,16},{1,25},{9,1},{17,9},{25,17},{2,26},{10... | collective-permute-start | bytes 7680008 | tf_op jit(solution)/shard_map/ppermute | solution.py:23
  533.8 218.1 %collective-permute-start.2 = (bf16[3200,400]{0,1:T(8,128)(2,1)}, bf16[3200,400]{0,1:T(8,128)(2,1)}, u32[]{:S(2)}, u32[]{:S(2)}) collective-permute-start(bf16[3200,400]{0,1:T(8,128)(2,1)} %collective-permute-done), channel_id=1, source_target_pairs={{0,8},{8,16},{16,24},{24,0},{1,9},{9,17},{17,25},{25,1},{2,10},{10... | collective-permute-start | bytes 7680008 | tf_op jit(solution)/shard_map/ppermute | solution.py:20
  755.4 28.3 copy-start.20
  755.4 28.3 copy-start.22
  758.1 74.1 %copy-start = (f32[1,256,1600]{1,2,0:T(8,128)}, f32[1,256,1600]{1,2,0:T(8,128)S(1)}, u32[]{:S(2)}) copy-start(f32[1,256,1600]{1,2,0:T(8,128)S(1)} %get-tuple-element.114) | copy-start | bytes 4915204
  758.3 32.9 %copy-start.11 = (bf16[1,256,1600]{1,2,0:T(8,128)(2,1)S(1)}, bf16[1,256,1600]{1,2,0:T(8,128)(2,1)}, u32[]{:S(2)}) copy-start(bf16[1,256,1600]{1,2,0:T(8,128)(2,1)} %param.21) | copy-start | bytes 2457604
  783.7 19.1 slice-start
  783.7 19.1 slice-start.1
  791.3 11.6 slice-start.2
  807.3 1061.1 %reduce-scatter.9.cloned.1.call-start = ((), (), s32[]{:S(2)}) async-start(), calls=%async_computation.7 | async-start | bytes 4259840 | tf_op jit(solution)/shard_map/reduce_scatter | solution.py:233
  807.4 11.1 copy-start.17
  881.7 1830.5 %all-reduce.24.cloned.1.call-start = ((), (), s32[]{:S(2)}) async-start(), calls=%async_computation.8 | async-start | bytes 3276800 | tf_op jit(solution)/shard_map/psum | solution.py:251
  1886.2 1392.3 %all-reduce.26.cloned.1.call-start = ((), (), s32[]{:S(2)}) async-start(), calls=%async_computation.9 | async-start | bytes 4481024 | tf_op jit(solution)/shard_map/psum | solution.py:282
  1897.6 10.8 copy-start.28
  2639.1 59.0 %collective-permute-start.3 = (bf16[60,4800]{1,0:T(8,128)(2,1)}, bf16[60,4800]{1,0:T(8,128)(2,1)}, u32[]{:S(2)}, u32[]{:S(2)}) collective-permute-start(bf16[60,4800]{1,0:T(8,128)(2,1)} %slice.41), channel_id=1, source_target_pairs={{0,2},{2,4},{4,6},{6,8},{8,10},{10,12},{12,14},{14,16},{16,18},{18... | collective-permute-start | bytes 1728008
  2650.5 23.8 copy-start.4
  2650.5 23.8 copy-start.15
  2652.8 549.9 %collective-permute-start.4 = (f32[112,3200]{1,0:T(8,128)}, f32[112,3200]{1,0:T(8,128)}, u32[]{:S(2)}, u32[]{:S(2)}) collective-permute-start(f32[112,3200]{1,0:T(8,128)} %get-tuple-element.111), channel_id=1, source_target_pairs={{0,2},{2,4},{4,6},{6,8},{8,10},{10,12},{12,14},{14,16},{16,18},{18... | collective-permute-start | bytes 4300808
  2657.0 560.3 %collective-permute-start.6 = (f32[3200,112]{0,1:T(8,128)S(1)}, f32[3200,112]{0,1:T(8,128)}, u32[]{:S(2)}, u32[]{:S(2)}) collective-permute-start(f32[3200,112]{0,1:T(8,128)S(1)} %get-tuple-element.112), channel_id=1, source_target_pairs={{0,2},{2,4},{4,6},{6,8},{8,10},{10,12},{12,14},{14,16},{16,18},{18... | collective-permute-start | bytes 4300808
  2659.5 557.8 %collective-permute-start.7 = (f32[3200,68]{0,1:T(8,128)}, f32[3200,68]{0,1:T(8,128)S(1)}, u32[]{:S(2)}, u32[]{:S(2)}) collective-permute-start(f32[3200,68]{0,1:T(8,128)} %slice.43), channel_id=1, source_target_pairs={{0,4},{2,6},{4,8},{6,10},{8,12},{10,14},{12,16},{14,18},{16,20},{1... | collective-permute-start | bytes 2611208
  2661.2 541.5 %collective-permute-start.5 = (f32[68,3200]{1,0:T(8,128)}, f32[68,3200]{1,0:T(8,128)}, u32[]{:S(2)}, u32[]{:S(2)}) collective-permute-start(f32[68,3200]{1,0:T(8,128)} %slice.42), channel_id=1, source_target_pairs={{0,4},{2,6},{4,8},{6,10},{8,12},{10,14},{12,16},{14,18},{16,20},{1... | collective-permute-start | bytes 2611208
  3234.6 43.8 %copy-start.1 = (f32[1,256,1600]{1,2,0:T(8,128)S(1)}, f32[1,256,1600]{1,2,0:T(8,128)}, u32[]{:S(2)}) copy-start(f32[1,256,1600]{1,2,0:T(8,128)} %copy-done) | copy-start | bytes 4915204
  (19 other events, 94.8 us)
Sparse Core Ops, SparseCore 0:
  9.6 269.6 all-gather.4
  280.8 97.5 all-gather.8
  380.8 44.2 all-gather.6
  449.3 20.4 all-reduce.19
  471.2 312.4 all-gather.10
  807.4 21.6 all-reduce.21
  881.8 161.7 reduce-scatter.8
  1886.3 26.6 all-reduce.23
  3202.2 76.1 all-reduce.25
